TPU v7x, 32 devices: a whole 2x2x4 slice. The times are simulated.
32 devices in a mesh: grp: 2 (over y), row: 4 (over x, core), col: 4 (over z).
Axes of the slice: x: 2, y: 2, z: 4, core: 2. Of those that a mesh axis runs over, the one named last changes fastest.
Arguments:
- perturbation: bfloat16 [4, 12000, 12000], P('grp', 'row', 'col'), parts along dimension 0, may hold values from -96 to 96
- occ_coeffs: bfloat16 [12000, 2000], P('row', 'col'), may hold values from -0.0546875 to 0.0546875
- vir_coeffs: bfloat16 [12000, 512], P('col', 'row'), may hold values from -0.0546875 to 0.0546875
- occ_energies: float32 [2000], replicated, may hold values from -1 to -0.1
- vir_energies: float32 [512], replicated, may hold values from 0.1 to 1.5
Outputs:
- density_response: bfloat16 [4, 12000, 12000], P('grp', 'row', 'col'), parts along dimension 0
There are 2 independent parts, one for each index of `grp`. A program takes and returns all parts, laid end to end along the dimension named above; an argument that names none is the same for every part. Nothing has to cross between parts.
All inputs are finite; a program needn't handle non-finite values.
Results may differ from a plain program's by a relative error of at most 0.0098.
Values may be sent and summed in bfloat16 or wider, within the bound.
A program may use at most 192 MiB of HBM per device.

v0:
```python
import jax
import jax.numpy as jnp
from jax import lax
from jax.sharding import PartitionSpec as P

BF16 = jnp.bfloat16
F32 = jnp.float32


def per_device(perturbation, occ_coeffs, vir_coeffs, occ_energies, vir_energies):
    vir_rows = lax.all_gather(vir_coeffs, "row", axis=1, tiled=True)
    occ_parts = lax.all_gather(occ_coeffs, "col")
    cols, _, width = occ_parts.shape
    image = jnp.einsum("pij,jv->piv", perturbation, vir_rows, preferred_element_type=F32).astype(
        BF16
    )
    part = jnp.einsum("cio,piv->pcov", occ_parts, image, preferred_element_type=F32).astype(BF16)
    coupling = lax.psum(part, ("row", "col"))
    gaps = occ_energies.reshape(cols, width)[:, :, None] - vir_energies[None, None, :]
    response = (coupling.astype(F32) / gaps[None]).astype(BF16)
    mixed = jnp.einsum("cio,pcov->piv", occ_parts, response, preferred_element_type=F32).astype(
        BF16
    )
    return jnp.einsum("piv,jv->pij", mixed, vir_rows, preferred_element_type=F32).astype(BF16)


def solution(mesh):
    placed = (P("grp", "row", "col"), P("row", "col"), P("col", "row"), P(), P())
    return jax.shard_map(
        per_device, mesh=mesh, in_specs=placed, out_specs=P("grp", "row", "col"), check_vma=False
    )
```

profile of v0, /device:TPU:0, one launch (start us, length us, event | category | flops | bytes accessed | tf_op | source)
XLA Modules:
  0.0 448.0 jit_solution(10581064769501468559)
XLA Ops:
  6.5 0.0 all-gather.4.cloned.1.call-start
  6.5 0.7 all-gather.4.cloned.1.call-update
  7.3 0.0 all-gather.6.cloned.1.call-start
  7.3 0.7 all-gather.6.cloned.1.call-update
  8.0 0.0 all-reduce.2.cloned.1.call-start
  8.1 32.1 %all-gather.4.cloned.1.call-done = bf16[3000,512]{1,0:T(8,128)(2,1)} async-done(((bf16[3000,128]{1,0:T(8,128)(2,1)}), bf16[3000,512]{1,0:T(8,128)(2,1)}) %all-gather.4.cloned.1.call-update) | async-done | bytes 3072016 | tf_op jit(solution)/shard_map/all_gather | solution.py:11
  40.1 25.8 %fusion.45 = bf16[2,3000,512,1]{2,1,3,0:T(8,128)(2,1)} fusion(bf16[2,3000,3000]{2,1,0:T(8,128)(2,1)} %param.5, bf16[3000,512]{1,0:T(8,128)(2,1)} %all-gather.4.cloned.1.call-done), kind=kOutput, calls=%fused_computation.5.clone.clone.clone.1 | convolution fusion | flops 18435072000 | bytes 45216000 | tf_op jit(solution)/shard_map/pij,jv->piv/dot_general | solution.py:14
  66.0 189.1 %all-gather.6.cloned.1.call-done = bf16[12000,500]{1,0:T(8,128)(2,1)} async-done(((bf16[3000,500]{1,0:T(8,128)(2,1)}), bf16[12000,500]{1,0:T(8,128)(2,1)}) %all-gather.6.cloned.1.call-update) | async-done | bytes 12000016 | tf_op jit(solution)/shard_map/all_gather | solution.py:12
  255.1 19.1 %fusion.17 = bf16[2,512,4,500]{1,3,2,0:T(8,128)(2,1)} fusion(bf16[4,3000,500,1]{2,1,0,3:T(8,128)(2,1)} %bitcast.58, bf16[2,3000,512,1]{2,1,3,0:T(8,128)(2,1)} %fusion.45), kind=kOutput, calls=%fused_computation.12 | convolution fusion | flops 12290048000 | bytes 22240000 | tf_op jit(solution)/shard_map/cio,piv->pcov/dot_general | solution.py:17
  274.2 0.0 copy-start
  274.2 0.0 copy-start.1
  274.2 7.8 %copy.10 = bf16[2,512,4,500]{3,2,1,0:T(4,128)(2,1)} copy(bf16[2,512,4,500]{1,3,2,0:T(8,128)(2,1)} %fusion.17) | data formatting | bytes 8192000
  282.0 0.0 all-reduce.2.cloned.1.call-update
  282.0 0.0 copy-done
  282.1 0.1 sub.19
  282.1 0.0 copy-done.1
  282.1 2.8 broadcast_subtract_fusion
  285.0 106.6 %all-reduce.2.cloned.1.call-done = bf16[2,4,500,512]{2,1,3,0:T(4,128)(2,1)} async-done(((bf16[2,4,500,512]{2,1,3,0:T(4,128)(2,1)}), bf16[2,4,500,512]{2,1,3,0:T(4,128)(2,1)}) %all-reduce.2.cloned.1.call-update) | async-done | bytes 4096016 | tf_op jit(solution)/shard_map/psum | solution.py:18
  391.5 5.5 %fusion = bf16[2,4,500,512]{2,1,3,0:T(4,128)(2,1)S(1)} fusion(bf16[2,4,500,512]{2,1,3,0:T(4,128)(2,1)} %all-reduce.2.cloned.1.call-done, f32[4,500,512]{1,0,2:T(4,128)} %broadcast_subtract_fusion), kind=kLoop, calls=%fused_computation.3 | loop fusion | flops 6144000 | bytes 12288000 | tf_op jit(solution)/shard_map/convert_element_type | solution.py:20
  397.1 16.8 %fusion.41 = bf16[2,3000,512]{2,1,0:T(8,128)(2,1)} fusion(bf16[4,3000,500,1]{2,1,0,3:T(8,128)(2,1)} %bitcast.59, bf16[2,4,500,512]{2,1,3,0:T(4,128)(2,1)S(1)} %fusion), kind=kOutput, calls=%fused_computation.6.clone.1 | convolution fusion | flops 12291072000 | bytes 22240000 | tf_op jit(solution)/shard_map/cio,pcov->piv/dot_general | solution.py:21
  413.9 27.6 %convolution_convert_fusion = bf16[2,3000,3000]{2,1,0:T(8,128)(2,1)} fusion(bf16[3000,512]{1,0:T(8,128)(2,1)} %all-gather.4.cloned.1.call-done, bf16[2,3000,512]{2,1,0:T(8,128)(2,1)} %fusion.41), kind=kOutput, calls=%fused_computation | convolution fusion | flops 18449999872 | bytes 45216000 | tf_op jit(solution)/shard_map/piv,jv->pij/dot_general | solution.py:24
Async XLA Ops:
  6.5 33.6 %all-gather.4.cloned.1.call-start = ((), (), s32[]{:S(2)}) async-start(), calls=%async_computation | async-start | bytes 3840000 | tf_op jit(solution)/shard_map/all_gather | solution.py:11
  7.3 247.8 %all-gather.6.cloned.1.call-start = ((), (), s32[]{:S(2)}) async-start(), calls=%async_computation.2 | async-start | bytes 15360000 | tf_op jit(solution)/shard_map/all_gather | solution.py:12
  8.0 383.5 %all-reduce.2.cloned.1.call-start = ((), (), s32[]{:S(2)}) async-start(), calls=%async_computation.1 | async-start | bytes 8388608 | tf_op jit(solution)/shard_map/psum | solution.py:18
  274.2 7.9 %copy-start = (f32[2000]{0:T(1024)S(1)}, f32[2000]{0:T(1024)}, u32[]{:S(2)}) copy-start(f32[2000]{0:T(1024)} %param.8) | copy-start | bytes 24004
  274.2 8.0 %copy-start.1 = (f32[512]{0:T(512)S(1)}, f32[512]{0:T(512)}, u32[]{:S(2)}) copy-start(f32[512]{0:T(512)} %param.9) | copy-start | bytes 6148
Sparse Core Ops, SparseCore 0:
  8.9 31.1 all-gather.3
  41.7 213.3 all-gather.5
  282.2 109.3 all-reduce.1
where the time goes:
time: 448 us
  waiting for transfers between devices  329 us (73%)
  matrix products  89.4 us (20%)
  between operations  13.1 us (3%)
  other arithmetic  8.38 us (2%)
  local copies, waits for them, and re-layouts  7.93 us (2%)
    all_gather x1, waiting for transfers between devices, per_device(): occ_parts = lax.all_gather(occ_coeffs, 'col')  189 us
    psum x1, waiting for transfers between devices, per_device(): coupling = lax.psum(part, ('row', 'col'))  107 us
    all_gather x1, waiting for transfers between devices, per_device(): vir_rows = lax.all_gather(vir_coeffs, 'row', axis=1, tiled=True)  32.1 us
    dot_general x1, matrix products, per_device(): jnp.einsum('piv,jv->pij', mixed, vir_rows, preferred_element_type=F32)  27.6 us
    dot_general x1, matrix products, per_device(): jnp.einsum('pij,jv->piv', perturbation, vir_rows, preferred_element_type=...  25.8 us
    dot_general x1, matrix products, per_device(): jnp.einsum('cio,piv->pcov', occ_parts, image, preferred_element_type=F32)  19.1 us
    dot_general x1, matrix products, per_device(): jnp.einsum('cio,pcov->piv', occ_parts, response, preferred_element_type=F32)  16.8 us
  transfers between devices with their start and end apart: 3, of which 3 were waited for; matrix products, arithmetic and copies ran while one was open for 6% of the time, Pallas kernels for 0%

commit v1 on v0

--- a/solution.py
+++ b/solution.py
@@ -2,6 +2,7 @@
 import jax.numpy as jnp
 from jax import lax
 from jax.sharding import PartitionSpec as P
+from jax.lax import all_gather
 
 BF16 = jnp.bfloat16
 F32 = jnp.float32
@@ -15,7 +16,11 @@
         BF16
     )
     part = jnp.einsum("cio,piv->pcov", occ_parts, image, preferred_element_type=F32).astype(BF16)
-    coupling = lax.psum(part, ("row", "col"))
+
+    def link_group(point, net_axis):
+        return all_gather(point, net_axis).sum(axis=0)
+
+    coupling = link_group(part, ("row", "col"))
     gaps = occ_energies.reshape(cols, width)[:, :, None] - vir_energies[None, None, :]
     response = (coupling.astype(F32) / gaps[None]).astype(BF16)
     mixed = jnp.einsum("cio,pcov->piv", occ_parts, response, preferred_element_type=F32).astype(

time: 448 us -> 705 us (1.57)
  waiting for transfers between devices: 329 us -> 556 us
  other arithmetic: 8.38 us -> 47.9 us
    all_gather x0 -> x1, waiting for transfers between devices: none -> 334 us  [link_group(): return all_gather(point, net_axis).sum(axis=0)]
    psum x1 -> x0, waiting for transfers between devices: 107 us -> none  [per_device(): coupling = lax.psum(part, ('row', 'col'))]
    reduce_sum x0 -> x1, other arithmetic: none -> 37.7 us  [link_group(): return all_gather(point, net_axis).sum(axis=0)]
    dot_general x1 -> x0, matrix products: 16.8 us -> none  [per_device(): jnp.einsum('cio,pcov->piv', occ_parts, response, preferred_element_type=F32)]
    dot_general x1, matrix products: 27.6 us -> 39.8 us  [per_device(): jnp.einsum('piv,jv->pij', mixed, vir_rows, preferred_element_type=F32)]
    unnamed x5 -> x6, local copies, waits for them, and re-layouts: 7.85 us -> 0.02 us
  transfers between devices with their start and end apart: 3 -> 3, of which waited for: 3 -> 3; matrix products, arithmetic and copies ran while one was open for 6% -> 4% of each run, Pallas kernels for 0% -> 0%
where the time goes in v1:
time: 705 us
  waiting for transfers between devices  556 us (79%)
  matrix products  82.9 us (12%)
  other arithmetic  47.9 us (7%)
  between operations  13.2 us (2%)
    all_gather x1, waiting for transfers between devices, link_group(): return all_gather(point, net_axis).sum(axis=0)  334 us
    all_gather x1, waiting for transfers between devices, per_device(): occ_parts = lax.all_gather(occ_coeffs, 'col')  189 us
    dot_general x1, matrix products, per_device(): jnp.einsum('piv,jv->pij', mixed, vir_rows, preferred_element_type=F32)  39.8 us
    reduce_sum x1, other arithmetic, link_group(): return all_gather(point, net_axis).sum(axis=0)  37.7 us
    all_gather x1, waiting for transfers between devices, per_device(): vir_rows = lax.all_gather(vir_coeffs, 'row', axis=1, tiled=True)  32.1 us
    dot_general x1, matrix products, per_device(): jnp.einsum('pij,jv->piv', perturbation, vir_rows, preferred_element_type=...  25.8 us
    dot_general x1, matrix products, per_device(): jnp.einsum('cio,piv->pcov', occ_parts, image, preferred_element_type=F32)  17.3 us
  transfers between devices with their start and end apart: 3, of which 3 were waited for; matrix products, arithmetic and copies ran while one was open for 4% of the time, Pallas kernels for 0%

profile of v1, /device:TPU:0, one launch (start us, length us, event | category | flops | bytes accessed | tf_op | source)
XLA Modules:
  0.0 704.9 jit_solution(371891771571585986)
XLA Ops:
  6.5 0.0 all-gather.6.cloned.1.call-start
  6.5 0.7 all-gather.6.cloned.1.call-update
  7.3 0.0 all-gather.8.cloned.1.call-start
  7.3 0.7 all-gather.8.cloned.1.call-update
  8.0 0.0 all-gather.10.cloned.1.call-start
  8.1 32.1 %all-gather.6.cloned.1.call-done = bf16[3000,512]{1,0:T(8,128)(2,1)} async-done(((bf16[3000,128]{1,0:T(8,128)(2,1)}), bf16[3000,512]{1,0:T(8,128)(2,1)}) %all-gather.6.cloned.1.call-update) | async-done | bytes 3072016 | tf_op jit(solution)/shard_map/all_gather | solution.py:12
  40.1 25.8 %fusion.40 = bf16[2,3000,512,1]{2,1,3,0:T(8,128)(2,1)} fusion(bf16[2,3000,3000]{2,1,0:T(8,128)(2,1)} %param.5, bf16[3000,512]{1,0:T(8,128)(2,1)} %all-gather.6.cloned.1.call-done), kind=kOutput, calls=%fused_computation.5.clone.clone.clone.1 | convolution fusion | flops 18435072000 | bytes 45216000 | tf_op jit(solution)/shard_map/pij,jv->piv/dot_general | solution.py:15
  65.9 189.2 %all-gather.8.cloned.1.call-done = bf16[12000,500]{1,0:T(8,128)(2,1)} async-done(((bf16[3000,500]{1,0:T(8,128)(2,1)}), bf16[12000,500]{1,0:T(8,128)(2,1)}) %all-gather.8.cloned.1.call-update) | async-done | bytes 12000016 | tf_op jit(solution)/shard_map/all_gather | solution.py:13
  255.1 17.3 %convert_bitcast_fusion = bf16[2,4,500,512]{3,2,1,0:T(8,128)(2,1)S(1)} fusion(bf16[4,3000,500,1]{2,1,0,3:T(8,128)(2,1)} %bitcast.57, bf16[2,3000,512,1]{2,1,3,0:T(8,128)(2,1)} %fusion.40), kind=kOutput, calls=%fused_computation.9 | convolution fusion | flops 12290048000 | bytes 22240000 | tf_op jit(solution)/shard_map/cio,piv->pcov/dot_general | solution.py:18
  272.4 0.0 copy-start
  272.4 0.0 copy-start.1
  272.4 4.1 copy.9
  276.5 0.0 all-gather.10.cloned.1.call-update
  276.5 0.0 copy-done
  276.5 0.1 sub.19
  276.6 0.1 copy.10
  276.8 0.0 copy-done.1
  276.8 2.8 broadcast_subtract_fusion
  279.6 333.8 %all-gather.10.cloned.1.call-done = bf16[32,4,500,512]{3,1,2,0:T(4,128)(2,1)} async-done(((bf16[2,4,500,512]{3,1,2,0:T(4,128)(2,1)}), bf16[32,4,500,512]{3,1,2,0:T(4,128)(2,1)}) %all-gather.10.cloned.1.call-update) | async-done | bytes 65536016 | tf_op jit(solution)/shard_map/all_gather | solution.py:21
  613.4 37.7 %reduce_sum.12 = bf16[2,4,500,512]{3,1,2,0:T(4,128)(2,1)} reduce(bf16[16,2,4,500,512]{4,2,3,1,0:T(4,128)(2,1)} %bitcast.56, bf16[]{:T(256)} %constant.2.clone.1), dimensions={0}, to_apply=%region_0.0 | reduce | flops 30720000 | bytes 69632000 | tf_op jit(solution)/shard_map/reduce_sum | solution.py:21
  651.1 0.0 copy-start.2
  651.1 7.5 %fusion = bf16[2,4,500,512]{3,1,2,0:T(4,128)(2,1)} fusion(bf16[2,4,500,512]{3,1,2,0:T(4,128)(2,1)} %reduce_sum.12, f32[4,500,512]{2,0,1:T(4,128)} %broadcast_subtract_fusion), kind=kLoop, calls=%fused_computation.3 | loop fusion | flops 6144000 | bytes 12288000 | tf_op jit(solution)/shard_map/convert_element_type | solution.py:25
  658.5 0.0 copy-done.2
  658.5 39.8 %convolution_convert_fusion = bf16[2,3000,3000]{2,1,0:T(8,128)(2,1)} fusion(bf16[4,3000,500,1]{2,1,0,3:T(8,128)(2,1)} %bitcast.58, bf16[2,4,500,512]{3,1,2,0:T(4,128)(2,1)} %fusion, bf16[3000,512]{1,0:T(8,128)(2,1)S(1)} %copy-done.2), kind=kOutput, calls=%fused_computation | convolution fusion | flops 30741071872 | bytes 55168000 | tf_op jit(solution)/shard_map/piv,jv->pij/dot_general | solution.py:29
Async XLA Ops:
  6.5 33.6 %all-gather.6.cloned.1.call-start = ((), (), s32[]{:S(2)}) async-start(), calls=%async_computation | async-start | bytes 3840000 | tf_op jit(solution)/shard_map/all_gather | solution.py:12
  7.3 247.8 %all-gather.8.cloned.1.call-start = ((), (), s32[]{:S(2)}) async-start(), calls=%async_computation.1 | async-start | bytes 15360000 | tf_op jit(solution)/shard_map/all_gather | solution.py:13
  8.0 605.4 %all-gather.10.cloned.1.call-start = ((), (), s32[]{:S(2)}) async-start(), calls=%async_computation.2 | async-start | bytes 69632000 | tf_op jit(solution)/shard_map/all_gather | solution.py:21
  272.4 4.1 copy-start
  272.4 4.4 copy-start.1
  651.1 7.5 %copy-start.2 = (bf16[3000,512]{1,0:T(8,128)(2,1)S(1)}, bf16[3000,512]{1,0:T(8,128)(2,1)}, u32[]{:S(2)}) copy-start(bf16[3000,512]{1,0:T(8,128)(2,1)} %all-gather.6.cloned.1.call-done) | copy-start | bytes 9216004
Sparse Core Ops, SparseCore 0:
  8.9 31.1 all-gather.5
  41.7 213.3 all-gather.7
  276.7 336.6 all-gather.9
